TPU v7x, 32 devices: a whole 2x2x4 slice. The times are simulated.
32 devices in a mesh: fsdp: 4 (over y, x), tenant: 4 (over z), dp: 2 (over core).
Axes of the slice: x: 2, y: 2, z: 4, core: 2. Of those that a mesh axis runs over, the one named last changes fastest.
Arguments:
- tokens: bfloat16 [3072, 5120], P(('fsdp', 'dp'), 'tenant'), may hold values from -6 to 6
- block_tenant_index: int32 [48], P(('fsdp', 'dp')), may hold values from 0 to 7
- ranks: int32 [8], replicated, may hold values from 16 to 64, as said below
- frozen_up_weight: bfloat16 [5120, 14336], P(('fsdp', 'dp'), 'tenant'), may hold values from -0.078125 to 0.078125
- tenant_down_adapters: bfloat16 [8, 64, 5120], P('tenant'), may hold values from -0.078125 to 0.078125
- tenant_up_adapters: bfloat16 [8, 64, 14336], P('tenant'), may hold values from -0.75 to 0.75
- cotangent: bfloat16 [3072, 14336], P(('fsdp', 'dp'), 'tenant'), may hold values from -6 to 6
Outputs:
- hidden_out: bfloat16 [3072, 14336], P(('fsdp', 'dp'), 'tenant')
- grad_tokens: bfloat16 [3072, 5120], P(('fsdp', 'dp'), 'tenant')
- grad_down: float32 [8, 64, 5120], P('dp', None, 'tenant')
- grad_up: float32 [8, 64, 14336], P('dp', None, 'tenant')
Inputs may be any that keep to these rules, and one draw needn't show every extreme that they name: `ranks`: multiples of 16; some tenant has rank 64.
All inputs are finite; a program needn't handle non-finite values.
Results may differ from a plain program's by a relative error of at most 0.0034.
Values may be sent and summed in bfloat16 or wider, within the bound.
No kernel may reach another device: no remote copies, remote signals or barrier semaphores. Data moves between devices by JAX's collectives and lax.ppermute only.
A program may use at most 128 MiB of HBM per device.

v0:
```python
import jax
import jax.numpy as jnp
from jax import lax
from jax.sharding import PartitionSpec as P

BLOCK = 64
alpha_scale = 32.0


def make_gain(block_tenant_index, ranks, rows, largest_rank):
    tenants = ranks.shape[0]
    rows_tenant = jnp.repeat(block_tenant_index, BLOCK, total_repeat_length=rows)
    columns = jnp.arange(tenants * largest_rank, dtype=jnp.int32)
    col_tenant = columns // largest_rank
    col_slot = columns % largest_rank
    ranks_col = jnp.repeat(ranks, largest_rank, total_repeat_length=tenants * largest_rank)
    keep = (rows_tenant[:, None] == col_tenant[None, :]) & (col_slot[None, :] < ranks_col[None, :])
    scale_col = alpha_scale / ranks_col.astype(jnp.float32)
    return jnp.where(keep, scale_col[None, :], jnp.float32(0.0))


def shards(
    tokens,
    block_tenant_index,
    ranks,
    frozen_up_weight,
    tenant_down_adapters,
    tenant_up_adapters,
    cotangent,
):
    rows = tokens.shape[0]
    local_d = tokens.shape[1]
    local_f = cotangent.shape[1]
    tenants = ranks.shape[0]
    largest_rank = tenant_down_adapters.shape[1]
    gain = make_gain(block_tenant_index, ranks, rows, largest_rank)
    whole = lax.all_gather(tokens, "tenant", axis=1, tiled=True)
    weight = lax.all_gather(frozen_up_weight, ("fsdp", "dp"), axis=0, tiled=True)
    down_part, up_adapter_slice = (
        lax.all_to_all(tenant_down_adapters, "tenant", split_axis=2, concat_axis=0, tiled=True),
        lax.all_to_all(tenant_up_adapters, "tenant", split_axis=2, concat_axis=0, tiled=True),
    )
    local_down = down_part.reshape(tenants * largest_rank, local_d)
    partial_proj = lax.dot_general(
        tokens, local_down, (((1,), (1,)), ((), ())), preferred_element_type=jnp.float32
    )
    proj = lax.psum(partial_proj, "tenant")
    flattened_up = up_adapter_slice.reshape(tenants * largest_rank, local_f)
    adapted = (proj * gain).astype(jnp.bfloat16)
    base = jnp.dot(whole, weight, preferred_element_type=jnp.float32)
    hidden_out = (base + jnp.dot(adapted, flattened_up, preferred_element_type=jnp.float32)).astype(
        jnp.bfloat16
    )
    back_part = lax.dot_general(
        cotangent, flattened_up, (((1,), (1,)), ((), ())), preferred_element_type=jnp.float32
    )
    back = lax.psum(back_part, "tenant")
    adapted_grad = (back * gain).astype(jnp.bfloat16)
    base_back = lax.dot_general(
        cotangent, weight, (((1,), (1,)), ((), ())), preferred_element_type=jnp.float32
    )
    grad_base = lax.psum_scatter(base_back, "tenant", scatter_dimension=1, tiled=True)
    grad_tokens = (
        grad_base + jnp.dot(adapted_grad, local_down, preferred_element_type=jnp.float32)
    ).astype(jnp.bfloat16)
    up_term = lax.dot_general(
        adapted, cotangent, (((0,), (0,)), ((), ())), preferred_element_type=jnp.float32
    )
    down_term = lax.dot_general(
        adapted_grad, tokens, (((0,), (0,)), ((), ())), preferred_element_type=jnp.float32
    )
    up_term = up_term.reshape(tenants, largest_rank, local_f)
    down_term = down_term.reshape(tenants, largest_rank, local_d)
    down_share, up_share = (
        lax.psum_scatter(down_term, "dp", scatter_dimension=0, tiled=True),
        lax.psum_scatter(up_term, "dp", scatter_dimension=0, tiled=True),
    )
    grad_down, grad_up = lax.psum((down_share, up_share), "fsdp")
    return (hidden_out, grad_tokens, grad_down, grad_up)


def solution(mesh):
    return jax.shard_map(
        shards,
        mesh=mesh,
        in_specs=(
            P(("fsdp", "dp"), "tenant"),
            P(("fsdp", "dp")),
            P(),
            P(("fsdp", "dp"), "tenant"),
            P("tenant", None, None),
            P("tenant", None, None),
            P(("fsdp", "dp"), "tenant"),
        ),
        out_specs=(
            P(("fsdp", "dp"), "tenant"),
            P(("fsdp", "dp"), "tenant"),
            P("dp", None, "tenant"),
            P("dp", None, "tenant"),
        ),
        check_vma=False,
    )
```

profile of v0, /device:TPU:0, one launch (start us, length us, event | category | flops | bytes accessed | tf_op | source)
XLA Modules:
  0.0 692.7 jit_solution(15375952981959615952)
XLA Ops:
  8.0 6.4 copy.13
  14.5 4.7 reshape.322
  19.1 6.3 all-to-all-start
  25.5 15.8 %copy.16 = bf16[2,64,14336]{1,0,2:T(2,128)(2,1)} copy(bf16[2,64,14336]{2,1,0:T(8,128)(2,1)} %param.16) | data formatting | bytes 7340032 | tf_op args[5]
  41.3 8.6 %reshape.320 = bf16[4,2,229376]{2,1,0:T(2,128)(2,1)} reshape(bf16[14336,2,64]{2,1,0:T(2,128)(2,1)} %bitcast.77) | data formatting | bytes 7340032
  49.9 7.1 %all-to-all-done = bf16[4,2,81920]{2,1,0:T(2,128)(2,1)} async-done(((bf16[4,2,81920]{2,1,0:T(2,128)(2,1)}), bf16[4,2,81920]{2,1,0:T(2,128)(2,1)}, u32[]{:S(2)}, u32[]{:S(2)}) %all-to-all-start) | async-done | bytes 1310752 | tf_op jit(solution)/shard_map/all_to_all | solution.py:40
  56.9 4.8 all-to-all-start.1
  61.8 4.6 reshape.323
  66.4 7.4 %copy.19 = bf16[2,64,4,1280]{3,2,1,0:T(4,128)(2,1)} copy(bf16[2,64,4,1280]{1,0,3,2:T(2,128)(2,1)} %bitcast.82) | data formatting | bytes 2621440 | tf_op jit(solution)/shard_map/all_to_all | solution.py:40
  73.8 1.4 copy.15
  76.3 2.8 fusion.26
  79.1 64.2 %all-to-all-done.1 = bf16[4,2,229376]{2,1,0:T(2,128)(2,1)} async-done(((bf16[4,2,229376]{2,1,0:T(2,128)(2,1)}), bf16[4,2,229376]{2,1,0:T(2,128)(2,1)}, u32[]{:S(2)}, u32[]{:S(2)}) %all-to-all-start.1) | async-done | bytes 3670048 | tf_op jit(solution)/shard_map/all_to_all | solution.py:41
  143.3 8.4 %reshape.321 = bf16[14336,2,64]{2,1,0:T(2,128)(2,1)} reshape(bf16[4,2,229376]{2,1,0:T(2,128)(2,1)} %all-to-all-done.1) | data formatting | bytes 7340032
  151.7 18.7 %copy.20 = bf16[2,64,4,3584]{3,2,1,0:T(4,128)(2,1)} copy(bf16[2,64,4,3584]{1,0,3,2:T(2,128)(2,1)} %bitcast.76) | data formatting | bytes 7340032 | tf_op jit(solution)/shard_map/all_to_all | solution.py:41
  170.4 2.7 copy.18
  173.1 1.8 copy-done.2
  174.9 2.5 fusion.28
  179.7 3.8 fusion.16
  183.5 4.5 compare_select_fusion.2
  188.9 56.8 %all-reduce.5.cloned.1.call-done = (f32[384,512]{1,0:T(8,128)}, f32[384,512]{1,0:T(8,128)}) async-done(((f32[384,512]{1,0:T(8,128)}, f32[384,512]{1,0:T(8,128)}), (f32[384,512]{1,0:T(8,128)}, f32[384,512]{1,0:T(8,128)})) %all-reduce.5.cloned.1.call-update) | async-done | bytes 1572880 | tf_op jit(solution)/shard_map/psum | solution.py:47
  245.7 4.0 fusion.17
  249.8 7.1 %fusion.20 = f32[512,3584]{1,0:T(8,128)} fusion(bf16[384,3584]{1,0:T(8,128)(2,1)S(1)} %copy-done, f32[384,512]{1,0:T(8,128)S(1)} %copy-done.5, f32[512]{0:T(512)S(1)} %convert_divide_fusion, s32[512]{0:T(512)S(1)} %add_select_fusion, s32[384]{0:T(512)S(1)} %and_select_fusion, pred[512]{0:T(512)(128)(4,1)S(1)} %get-tuple-element.32), kind=kOutput, calls=%fused_computation.52 | convolution fusion | flops 1410269184 | bytes 10885120 | tf_op jit(solution)/shard_map/dot_general | solution.py:66
  257.7 96.2 %all-gather.5.cloned.1.call-done = bf16[5120,3584]{1,0:T(8,128)(2,1)} async-done(((bf16[640,3584]{1,0:T(8,128)(2,1)}), bf16[5120,3584]{1,0:T(8,128)(2,1)}) %all-gather.5.cloned.1.call-update) | async-done | bytes 36700176 | tf_op jit(solution)/shard_map/all_gather | solution.py:38
  353.9 22.1 %fusion.27 = f32[384,5120]{1,0:T(8,128)} fusion(bf16[384,3584]{1,0:T(8,128)(2,1)S(1)} %copy-done, bf16[5120,3584]{1,0:T(8,128)(2,1)} %all-gather.5.cloned.1.call-done), kind=kOutput, calls=%fused_computation.57 | convolution fusion | flops 14092861440 | bytes 47316992 | tf_op jit(solution)/shard_map/dot_general | solution.py:59
  376.6 139.9 %all-gather.3.cloned.1.call-done = bf16[384,5120]{1,0:T(8,128)(2,1)} async-done(((bf16[384,1280]{1,0:T(8,128)(2,1)}), bf16[384,5120]{1,0:T(8,128)(2,1)}) %all-gather.3.cloned.1.call-update) | async-done | bytes 3932176 | tf_op jit(solution)/shard_map/all_gather | solution.py:37
  516.5 23.5 %fusion.25 = f32[384,3584]{1,0:T(8,128)} fusion(bf16[384,5120]{1,0:T(8,128)(2,1)} %all-gather.3.cloned.1.call-done, bf16[5120,3584]{1,0:T(8,128)(2,1)} %all-gather.5.cloned.1.call-done), kind=kOutput, calls=%fused_computation.55 | convolution fusion | flops 14092861440 | bytes 46137344 | tf_op jit(solution)/shard_map/dot_general | solution.py:50
  540.0 7.0 %fusion = bf16[384,3584]{1,0:T(8,128)(2,1)} fusion(f32[384,3584]{1,0:T(8,128)} %fusion.25, bf16[512,3584]{1,0:T(8,128)(2,1)} %bitcast.79, f32[384,512]{1,0:T(8,128)S(1)} %copy-done.5, f32[512]{0:T(512)S(1)} %convert_divide_fusion, s32[512]{0:T(512)S(1)} %add_select_fusion, s32[384]{0:T(512)S(1)} %and_select_fusion, pred[512]{0:T(512)(128)(4,1)S(1)} %get-tuple-element.32), kind=kOutput, calls=%fused_computation.1 | convolution fusion | flops 1413021696 | bytes 12720128 | tf_op jit(solution)/shard_map/dot_general | solution.py:51
  547.0 10.7 %reduce-scatter.4.cloned.1.call-done = f32[384,1280]{1,0:T(8,128)} async-done(((f32[384,5120]{1,0:T(8,128)}), f32[384,1280]{1,0:T(8,128)}) %reduce-scatter.4.cloned.1.call-update) | async-done | bytes 1966096 | tf_op jit(solution)/shard_map/reduce_scatter | solution.py:62
  557.7 3.3 fusion.1
  561.0 117.8 %all-reduce.7.cloned.1.call-done = (f32[4,64,1280]{2,1,0:T(8,128)}, f32[4,64,3584]{2,1,0:T(8,128)}) async-done(((f32[4,64,1280]{2,1,0:T(8,128)}, f32[4,64,3584]{2,1,0:T(8,128)}), (f32[4,64,1280]{2,1,0:T(8,128)}, f32[4,64,3584]{2,1,0:T(8,128)})) %all-reduce.7.cloned.1.call-update) | async-done | bytes 4980752 | tf_op jit(solution)/shard_map/psum | solution.py:78
  678.8 2.6 copy.29
  681.4 4.1 copy.30
  (48 shorter events, 5.6 us)
Async XLA Ops:
  8.0 166.9 %copy-start = (bf16[384,3584]{1,0:T(8,128)(2,1)S(1)}, bf16[384,3584]{1,0:T(8,128)(2,1)}, u32[]{:S(2)}) copy-start(bf16[384,3584]{1,0:T(8,128)(2,1)} %param.17) | copy-start | bytes 8257540
  19.1 37.8 %all-to-all-start = ((bf16[4,2,81920]{2,1,0:T(2,128)(2,1)}), bf16[4,2,81920]{2,1,0:T(2,128)(2,1)}, u32[]{:S(2)}, u32[]{:S(2)}) async-start(bf16[4,2,81920]{2,1,0:T(2,128)(2,1)} %reshape.322), calls=%async_computation | async-start | bytes 2621440 | tf_op jit(solution)/shard_map/all_to_all | solution.py:40
  56.9 86.3 %all-to-all-start.1 = ((bf16[4,2,229376]{2,1,0:T(2,128)(2,1)}), bf16[4,2,229376]{2,1,0:T(2,128)(2,1)}, u32[]{:S(2)}, u32[]{:S(2)}) async-start(bf16[4,2,229376]{2,1,0:T(2,128)(2,1)} %reshape.320), calls=%async_computation.1 | async-start | bytes 7340032 | tf_op jit(solution)/shard_map/all_to_all | solution.py:41
  61.8 184.0 %all-reduce.5.cloned.1.call-start = ((), (), s32[]{:S(2)}) async-start(), calls=%async_computation.10 | async-start | bytes 3145728 | tf_op jit(solution)/shard_map/psum | solution.py:47
  75.3 1.1 copy-start.3
  173.1 1.8 copy-start.2
  177.4 0.7 copy-start.8
  177.4 1.4 copy-start.7
  177.4 2.1 copy-start.10
  177.4 2.2 copy-start.9
  177.5 176.5 %all-gather.5.cloned.1.call-start = ((), (), s32[]{:S(2)}) async-start(), calls=%async_computation.6 | async-start | bytes 41287680 | tf_op jit(solution)/shard_map/all_gather | solution.py:38
  178.0 198.0 %reduce-scatter.6.cloned.1.call-start = ((), (), s32[]{:S(2)}) async-start(), calls=%async_computation.8 | async-start | bytes 3932160 | tf_op jit(solution)/shard_map/reduce_scatter | solution.py:75
  245.7 4.1 copy-start.5
  249.7 126.4 %reduce-scatter.8.cloned.1.call-start = ((), (), s32[]{:S(2)}) async-start(), calls=%async_computation.9 | async-start | bytes 11010048 | tf_op jit(solution)/shard_map/reduce_scatter | solution.py:76
  256.9 259.6 %all-gather.3.cloned.1.call-start = ((), (), s32[]{:S(2)}) async-start(), calls=%async_computation.5 | async-start | bytes 4915200 | tf_op jit(solution)/shard_map/all_gather | solution.py:37
  257.5 300.2 %reduce-scatter.4.cloned.1.call-start = ((), (), s32[]{:S(2)}) async-start(), calls=%async_computation.7 | async-start | bytes 9830400 | tf_op jit(solution)/shard_map/reduce_scatter | solution.py:62
  376.0 302.8 %all-reduce.7.cloned.1.call-start = ((), (), s32[]{:S(2)}) async-start(), calls=%async_computation.11 | async-start | bytes 9961472 | tf_op jit(solution)/shard_map/psum | solution.py:78
  540.0 17.8 %copy-start.4 = (bf16[4,2,64,1280]{3,2,1,0:T(8,128)(2,1)S(1)}, bf16[4,2,64,1280]{3,2,1,0:T(8,128)(2,1)}, u32[]{:S(2)}) copy-start(bf16[4,2,64,1280]{3,2,1,0:T(8,128)(2,1)} %copy-done.3) | copy-start | bytes 3932164
  540.0 17.8 %copy-start.6 = (f32[384,512]{1,0:T(8,128)S(1)}, f32[384,512]{1,0:T(8,128)}, u32[]{:S(2)}) copy-start(f32[384,512]{1,0:T(8,128)} %get-tuple-element.29) | copy-start | bytes 2359300
  678.8 6.8 copy-start.1
Sparse Core Ops, SparseCore 0:
  177.6 68.0 all-reduce.4
  249.9 16.8 reduce-scatter.5
  269.1 17.2 reduce-scatter.7
  376.1 181.5 reduce-scatter.3
  561.2 117.5 all-reduce.6
Sparse Core Ops, SparseCore 1:
  179.9 174.0 all-gather.4
  355.4 161.1 all-gather.2
where the time goes:
time: 695 us; the launch traced here: 693 us
  waiting for transfers between devices  494 us (71%)
  local copies, waits for them, and re-layouts  89.8 us (13%)
  matrix products  72.2 us (10%)
  between operations  15.4 us (2%)
  starting transfers between devices  11.6 us (2%)
  other arithmetic  9.35 us (1%)
    all_gather x1, waiting for transfers between devices, shards(): whole = lax.all_gather(tokens, 'tenant', axis=1, tiled=True)  140 us
    psum x1, waiting for transfers between devices, shards(): grad_down, grad_up = lax.psum((down_share, up_share), 'fsdp')  118 us
    all_gather x1, waiting for transfers between devices, shards(): lax.all_gather(frozen_up_weight, ('fsdp', 'dp'), axis=0, tiled=True)  96.2 us
    all_to_all x1, waiting for transfers between devices, shards(): lax.all_to_all(tenant_up_adapters, 'tenant', split_axis=2, concat_axis=0,...  64.2 us
    unnamed x30, local copies, waits for them, and re-layouts  58.2 us
    psum x1, waiting for transfers between devices, shards(): proj = lax.psum(partial_proj, 'tenant')  56.8 us
    dot_general x1, matrix products, shards(): base = jnp.dot(whole, weight, preferred_element_type=jnp.float32)  23.5 us
    dot_general x1, matrix products, shards(): lax.dot_general(cotangent, weight, (((1,), (1,)), ((), ())), preferred_el...  22.1 us
  transfers between devices with their start and end apart: 9, of which 7 were waited for; matrix products, arithmetic and copies ran while one was open for 17% of the time, Pallas kernels for 0%

commit v1 on v0

--- a/solution.py
+++ b/solution.py
@@ -5,6 +5,12 @@
 
 BLOCK = 64
 alpha_scale = 32.0
+
+
+def exchange_blocks(x, axis, split, join):
+    pieces = jnp.split(x, lax.axis_size(axis), axis=split)
+    arrived = lax.all_to_all(jnp.stack(pieces), axis, 0, 0)
+    return jnp.concatenate(arrived, axis=join)
 
 
 def make_gain(block_tenant_index, ranks, rows, largest_rank):
@@ -38,7 +44,7 @@
     weight = lax.all_gather(frozen_up_weight, ("fsdp", "dp"), axis=0, tiled=True)
     down_part, up_adapter_slice = (
         lax.all_to_all(tenant_down_adapters, "tenant", split_axis=2, concat_axis=0, tiled=True),
-        lax.all_to_all(tenant_up_adapters, "tenant", split_axis=2, concat_axis=0, tiled=True),
+        exchange_blocks(tenant_up_adapters, "tenant", 2, 0),
     )
     local_down = down_part.reshape(tenants * largest_rank, local_d)
     partial_proj = lax.dot_general(

time: 695 us -> 664 us (0.955)
  local copies, waits for them, and re-layouts: 89.8 us -> 36.2 us
  waiting for transfers between devices: 494 us -> 514 us
    unnamed x30 -> x25, local copies, waits for them, and re-layouts: 58.2 us -> 23.6 us
    all_to_all x2 -> x0, local copies, waits for them, and re-layouts: 21.4 us -> none  [shards(): lax.all_to_all(tenant_up_adapters, 'tenant', split_axis=2, concat_axis=0,...]
    all_to_all x1, waiting for transfers between devices: 7.06 us -> 27 us  [shards(): lax.all_to_all(tenant_down_adapters, 'tenant', split_axis=2, concat_axis=...]
  transfers between devices with their start and end apart: 9 -> 9, of which waited for: 7 -> 7; matrix products, arithmetic and copies ran while one was open for 17% -> 15% of each run, Pallas kernels for 0% -> 0%
where the time goes in v1:
time: 664 us; the launch traced here: 663 us
  waiting for transfers between devices  514 us (77%)
  matrix products  74.2 us (11%)
  local copies, waits for them, and re-layouts  36.2 us (5%)
  between operations  15.4 us (2%)
  starting transfers between devices  11.6 us (2%)
  other arithmetic  11.3 us (2%)
    all_gather x1, waiting for transfers between devices, shards(): whole = lax.all_gather(tokens, 'tenant', axis=1, tiled=True)  140 us
    psum x1, waiting for transfers between devices, shards(): grad_down, grad_up = lax.psum((down_share, up_share), 'fsdp')  118 us
    all_gather x1, waiting for transfers between devices, shards(): lax.all_gather(frozen_up_weight, ('fsdp', 'dp'), axis=0, tiled=True)  96.4 us
    all_to_all x1, waiting for transfers between devices, exchange_blocks(): arrived = lax.all_to_all(jnp.stack(pieces), axis, 0, 0)  64.2 us
    psum x1, waiting for transfers between devices, shards(): proj = lax.psum(partial_proj, 'tenant')  57 us
    all_to_all x1, waiting for transfers between devices, shards(): lax.all_to_all(tenant_down_adapters, 'tenant', split_axis=2, concat_axis=...  27 us
    unnamed x25, local copies, waits for them, and re-layouts  23.6 us
    dot_general x1, matrix products, shards(): base = jnp.dot(whole, weight, preferred_element_type=jnp.float32)  23.5 us
  transfers between devices with their start and end apart: 9, of which 7 were waited for; matrix products, arithmetic and copies ran while one was open for 15% of the time, Pallas kernels for 0%

profile of v1, /device:TPU:0, one launch (start us, length us, event | category | flops | bytes accessed | tf_op | source)
XLA Modules:
  0.0 663.0 jit_solution(16354701321059353911)
XLA Ops:
  8.0 6.4 copy.15
  14.5 4.7 reshape.315
  19.1 6.3 all-to-all-start
  25.5 2.4 slice_bitcast_fusion.3
  27.9 2.1 pad_maximum_fusion
  29.9 27.0 %all-to-all-done = bf16[4,2,81920]{2,1,0:T(2,128)(2,1)} async-done(((bf16[4,2,81920]{2,1,0:T(2,128)(2,1)}), bf16[4,2,81920]{2,1,0:T(2,128)(2,1)}, u32[]{:S(2)}, u32[]{:S(2)}) %all-to-all-start) | async-done | bytes 1310752 | tf_op jit(solution)/shard_map/all_to_all | solution.py:46
  56.9 4.8 all-to-all-start.1
  61.8 4.6 reshape.316
  66.4 7.4 %copy.20 = bf16[2,64,4,1280]{3,2,1,0:T(4,128)(2,1)} copy(bf16[2,64,4,1280]{1,0,3,2:T(2,128)(2,1)} %bitcast.83) | data formatting | bytes 2621440 | tf_op jit(solution)/shard_map/all_to_all | solution.py:46
  73.8 1.4 copy.17
  75.2 1.0 copy-done.2
  76.3 2.8 fusion.26
  79.1 64.2 %all-to-all-done.1 = bf16[4,2,64,3584]{3,2,1,0:T(8,128)(2,1)} async-done(((bf16[4,2,64,3584]{3,2,1,0:T(8,128)(2,1)}), bf16[4,2,64,3584]{3,2,1,0:T(8,128)(2,1)}, u32[]{:S(2)}, u32[]{:S(2)}) %all-to-all-start.1) | async-done | bytes 3670048 | tf_op jit(solution)/shard_map/all_to_all | solution.py:12
  143.2 4.5 convolution_bitcast_fusion
  148.5 0.7 fusion.23
  149.1 0.7 fusion.24
  150.0 3.9 fusion.16
  153.9 4.3 compare_select_fusion.2
  158.2 0.7 fusion.12
  159.0 57.0 %all-reduce.5.cloned.1.call-done = (f32[384,512]{1,0:T(8,128)}, f32[384,512]{1,0:T(8,128)}) async-done(((f32[384,512]{1,0:T(8,128)}, f32[384,512]{1,0:T(8,128)}), (f32[384,512]{1,0:T(8,128)}, f32[384,512]{1,0:T(8,128)})) %all-reduce.5.cloned.1.call-update) | async-done | bytes 1572880 | tf_op jit(solution)/shard_map/psum | solution.py:53
  216.0 4.0 fusion.17
  220.1 7.1 %fusion.20 = f32[512,3584]{1,0:T(8,128)} fusion(bf16[384,3584]{1,0:T(8,128)(2,1)S(1)} %copy-done, f32[384,512]{1,0:T(8,128)S(1)} %copy-done.4, f32[512]{0:T(512)S(1)} %convert_divide_fusion, s32[512]{0:T(512)S(1)} %add_select_fusion, s32[384]{0:T(512)S(1)} %and_select_fusion, pred[512]{0:T(512)(128)(4,1)S(1)} %get-tuple-element.32), kind=kOutput, calls=%fused_computation.58 | convolution fusion | flops 1410269184 | bytes 10885120 | tf_op jit(solution)/shard_map/dot_general | solution.py:72
  227.9 96.4 %all-gather.5.cloned.1.call-done = bf16[5120,3584]{1,0:T(8,128)(2,1)} async-done(((bf16[640,3584]{1,0:T(8,128)(2,1)}), bf16[5120,3584]{1,0:T(8,128)(2,1)}) %all-gather.5.cloned.1.call-update) | async-done | bytes 36700176 | tf_op jit(solution)/shard_map/all_gather | solution.py:44
  324.3 22.1 %fusion.27 = f32[384,5120]{1,0:T(8,128)} fusion(bf16[384,3584]{1,0:T(8,128)(2,1)S(1)} %copy-done, bf16[5120,3584]{1,0:T(8,128)(2,1)} %all-gather.5.cloned.1.call-done), kind=kOutput, calls=%fused_computation.63 | convolution fusion | flops 14092861440 | bytes 47316992 | tf_op jit(solution)/shard_map/dot_general | solution.py:65
  347.0 139.9 %all-gather.3.cloned.1.call-done = bf16[384,5120]{1,0:T(8,128)(2,1)} async-done(((bf16[384,1280]{1,0:T(8,128)(2,1)}), bf16[384,5120]{1,0:T(8,128)(2,1)}) %all-gather.3.cloned.1.call-update) | async-done | bytes 3932176 | tf_op jit(solution)/shard_map/all_gather | solution.py:43
  486.8 23.5 %fusion.25 = f32[384,3584]{1,0:T(8,128)} fusion(bf16[384,5120]{1,0:T(8,128)(2,1)} %all-gather.3.cloned.1.call-done, bf16[5120,3584]{1,0:T(8,128)(2,1)} %all-gather.5.cloned.1.call-done), kind=kOutput, calls=%fused_computation.61 | convolution fusion | flops 14092861440 | bytes 46137344 | tf_op jit(solution)/shard_map/dot_general | solution.py:56
  510.3 7.0 %fusion = bf16[384,3584]{1,0:T(8,128)(2,1)} fusion(f32[384,3584]{1,0:T(8,128)} %fusion.25, bf16[512,3584]{1,0:T(8,128)(2,1)} %bitcast.28, f32[384,512]{1,0:T(8,128)S(1)} %copy-done.4, f32[512]{0:T(512)S(1)} %convert_divide_fusion, s32[512]{0:T(512)S(1)} %add_select_fusion, s32[384]{0:T(512)S(1)} %and_select_fusion, pred[512]{0:T(512)(128)(4,1)S(1)} %get-tuple-element.32), kind=kOutput, calls=%fused_computation.1 | convolution fusion | flops 1413021696 | bytes 12720128 | tf_op jit(solution)/shard_map/dot_general | solution.py:57
  517.3 10.7 %reduce-scatter.4.cloned.1.call-done = f32[384,1280]{1,0:T(8,128)} async-done(((f32[384,5120]{1,0:T(8,128)}), f32[384,1280]{1,0:T(8,128)}) %reduce-scatter.4.cloned.1.call-update) | async-done | bytes 1966096 | tf_op jit(solution)/shard_map/reduce_scatter | solution.py:68
  528.1 3.3 fusion.1
  531.4 117.8 %all-reduce.7.cloned.1.call-done = (f32[4,64,1280]{2,1,0:T(8,128)}, f32[4,64,3584]{2,1,0:T(8,128)}) async-done(((f32[4,64,1280]{2,1,0:T(8,128)}, f32[4,64,3584]{2,1,0:T(8,128)}), (f32[4,64,1280]{2,1,0:T(8,128)}, f32[4,64,3584]{2,1,0:T(8,128)})) %all-reduce.7.cloned.1.call-update) | async-done | bytes 4980752 | tf_op jit(solution)/shard_map/psum | solution.py:84
  649.1 2.6 copy.29
  651.8 4.1 copy.30
  (43 shorter events, 2.2 us)
Async XLA Ops:
  8.0 135.2 %copy-start = (bf16[384,3584]{1,0:T(8,128)(2,1)S(1)}, bf16[384,3584]{1,0:T(8,128)(2,1)}, u32[]{:S(2)}) copy-start(bf16[384,3584]{1,0:T(8,128)(2,1)} %param.17) | copy-start | bytes 8257540
  19.1 37.8 %all-to-all-start = ((bf16[4,2,81920]{2,1,0:T(2,128)(2,1)}), bf16[4,2,81920]{2,1,0:T(2,128)(2,1)}, u32[]{:S(2)}, u32[]{:S(2)}) async-start(bf16[4,2,81920]{2,1,0:T(2,128)(2,1)} %reshape.315), calls=%async_computation | async-start | bytes 2621440 | tf_op jit(solution)/shard_map/all_to_all | solution.py:46
  56.9 86.3 %all-to-all-start.1 = ((bf16[4,2,64,3584]{3,2,1,0:T(8,128)(2,1)}), bf16[4,2,64,3584]{3,2,1,0:T(8,128)(2,1)}, u32[]{:S(2)}, u32[]{:S(2)}) async-start(bf16[4,2,64,3584]{3,2,1,0:T(8,128)(2,1)} %pad_maximum_fusion), calls=%async_computation.1 | async-start | bytes 7340032 | tf_op jit(solution)/shard_map/all_to_all | solution.py:12
  61.7 154.3 %all-reduce.5.cloned.1.call-start = ((), (), s32[]{:S(2)}) async-start(), calls=%async_computation.10 | async-start | bytes 3145728 | tf_op jit(solution)/shard_map/psum | solution.py:53
  75.2 1.1 copy-start.2
  147.8 0.7 copy-start.7
  147.8 1.4 copy-start.6
  147.8 2.1 copy-start.9
  147.8 2.2 copy-start.8
  147.8 176.5 %all-gather.5.cloned.1.call-start = ((), (), s32[]{:S(2)}) async-start(), calls=%async_computation.6 | async-start | bytes 41287680 | tf_op jit(solution)/shard_map/all_gather | solution.py:44
  148.4 198.2 %reduce-scatter.6.cloned.1.call-start = ((), (), s32[]{:S(2)}) async-start(), calls=%async_computation.8 | async-start | bytes 3932160 | tf_op jit(solution)/shard_map/reduce_scatter | solution.py:81
  216.0 4.1 copy-start.4
  220.1 126.6 %reduce-scatter.8.cloned.1.call-start = ((), (), s32[]{:S(2)}) async-start(), calls=%async_computation.9 | async-start | bytes 11010048 | tf_op jit(solution)/shard_map/reduce_scatter | solution.py:82
  227.2 259.6 %all-gather.3.cloned.1.call-start = ((), (), s32[]{:S(2)}) async-start(), calls=%async_computation.5 | async-start | bytes 4915200 | tf_op jit(solution)/shard_map/all_gather | solution.py:43
  227.8 300.3 %reduce-scatter.4.cloned.1.call-start = ((), (), s32[]{:S(2)}) async-start(), calls=%async_computation.7 | async-start | bytes 9830400 | tf_op jit(solution)/shard_map/reduce_scatter | solution.py:68
  346.4 302.8 %all-reduce.7.cloned.1.call-start = ((), (), s32[]{:S(2)}) async-start(), calls=%async_computation.11 | async-start | bytes 9961472 | tf_op jit(solution)/shard_map/psum | solution.py:84
  510.3 17.8 %copy-start.3 = (bf16[4,2,64,1280]{3,2,1,0:T(8,128)(2,1)S(1)}, bf16[4,2,64,1280]{3,2,1,0:T(8,128)(2,1)}, u32[]{:S(2)}) copy-start(bf16[4,2,64,1280]{3,2,1,0:T(8,128)(2,1)} %copy-done.2) | copy-start | bytes 3932164
  510.3 17.8 %copy-start.5 = (f32[384,512]{1,0:T(8,128)S(1)}, f32[384,512]{1,0:T(8,128)}, u32[]{:S(2)}) copy-start(f32[384,512]{1,0:T(8,128)} %get-tuple-element.29) | copy-start | bytes 2359300
  649.1 6.8 %copy-start.1 = (bf16[384,3584]{1,0:T(8,128)(2,1)S(1)}, bf16[384,3584]{1,0:T(8,128)(2,1)}, u32[]{:S(2)}) copy-start(bf16[384,3584]{1,0:T(8,128)(2,1)} %param.17) | copy-start | bytes 8257540
Sparse Core Ops, SparseCore 0:
  147.9 68.0 all-reduce.4
  220.2 16.8 reduce-scatter.5
  239.4 17.3 reduce-scatter.7
  346.5 181.5 reduce-scatter.3
  531.5 117.5 all-reduce.6
Sparse Core Ops, SparseCore 1:
  150.2 174.0 all-gather.4
  325.7 161.1 all-gather.2
